TPU v7x, 32 devices: a whole 2x2x4 slice. The times are simulated.
32 devices in a mesh: dp: 16 (over z, y, x), mp: 2 (over core).
Axes of the slice: x: 2, y: 2, z: 4, core: 2. Of those that a mesh axis runs over, the one named last changes fastest.
Arguments:
- inputs: bfloat16 [2048, 1792], P('dp', 'mp'), may hold values from -6 to 6
- cotangent: bfloat16 [2048, 1792], P('dp', 'mp'), may hold values from -6 to 6
- gate_weight: bfloat16 [9472, 1792], P(('mp', 'dp')), may hold values from -0.125 to 0.125
- up_weight: bfloat16 [9472, 1792], P(('mp', 'dp')), may hold values from -0.125 to 0.125
- down_weight: bfloat16 [9472, 1792], P(('mp', 'dp')), may hold values from -0.0625 to 0.0625
Outputs:
- input_grad: bfloat16 [2048, 1792], P('dp', 'mp')
- gate_grad: bfloat16 [9472, 1792], P(('mp', 'dp'))
All inputs are finite; a program needn't handle non-finite values.
Results may differ from a plain program's by a relative error of at most 0.009.
Values may be sent and summed in bfloat16 or wider, within the bound.
A program may use at most 320 MiB of HBM per device.

v0:
```python
import jax
import jax.numpy as jnp
from jax import lax
from jax.sharding import PartitionSpec as P


def tdot(left, right):
    return lax.dot_general(
        left, right, (((0,), (0,)), ((), ())), preferred_element_type=jnp.float32
    )


def rdot(left, right):
    return lax.dot_general(
        left, right, (((1,), (1,)), ((), ())), preferred_element_type=jnp.float32
    )


def per_device(inputs, cotangent, gate_weight, up_weight, down_weight):
    full_in, full_cot = (
        lax.all_gather(inputs, "mp", axis=1, tiled=True),
        lax.all_gather(cotangent, "mp", axis=1, tiled=True),
    )
    pieces = lax.all_gather((gate_weight, up_weight), "dp", axis=0, tiled=True)
    stacked = jnp.stack([rdot(full_in, pieces[0]), rdot(full_in, pieces[1])])
    gate = stacked[0]
    up = stacked[1]
    dhidden = rdot(full_cot, lax.all_gather(down_weight, "dp", axis=0, tiled=True))
    sig = jax.nn.sigmoid(gate)
    act = gate * sig
    dup = (dhidden * act).astype(jnp.bfloat16)
    dgate = (dhidden * up * sig * (1.0 + gate * (1.0 - sig))).astype(jnp.bfloat16)
    owned = lax.all_to_all(dgate, "dp", split_axis=1, concat_axis=0, tiled=True)
    gate_sum = tdot(owned, lax.all_gather(full_in, "dp", axis=0, tiled=True))
    pieces = (
        lax.all_gather(gate_weight, "dp", axis=0, tiled=True),
        lax.all_gather(up_weight, "dp", axis=0, tiled=True),
    )
    total = jnp.dot(dgate, pieces[0], preferred_element_type=jnp.float32)
    partial_value = total + jnp.dot(dup, pieces[1], preferred_element_type=jnp.float32)
    input_grad = lax.psum_scatter(
        partial_value.astype(jnp.bfloat16), "mp", scatter_dimension=1, tiled=True
    )
    gate_grad = gate_sum.astype(jnp.bfloat16)
    return (input_grad, gate_grad)


def solution(mesh):
    placed = (
        P("dp", "mp"),
        P("dp", "mp"),
        P(("mp", "dp"), None),
        P(("mp", "dp"), None),
        P(("mp", "dp"), None),
    )
    return jax.shard_map(
        per_device,
        mesh=mesh,
        in_specs=placed,
        out_specs=(P("dp", "mp"), P(("mp", "dp"), None)),
        check_vma=False,
    )
```

profile of v0, /device:TPU:0, one launch (start us, length us, event | category | flops | bytes accessed | tf_op | source)
XLA Modules:
  0.0 756.9 jit_solution(10167168134692143679)
XLA Ops:
  7.2 0.0 copy-start.3
  7.2 0.0 copy-start.4
  7.2 0.0 all-gather.9.cloned.1.call-start
  7.2 0.7 all-gather.9.cloned.1.call-update
  7.9 0.0 all-gather.5.cloned.1.call-start
  8.0 0.7 all-gather.5.cloned.1.call-update
  8.7 0.0 all-gather.7.cloned.1.call-start
  8.7 0.7 all-gather.7.cloned.1.call-update
  9.4 0.0 reduce-scatter.4.cloned.1.call-start
  9.4 0.0 copy-done.3
  9.5 2.3 all_gather.22
  11.7 0.0 copy-start
  11.7 0.0 copy-done.4
  11.7 2.1 all_gather.20
  13.8 192.5 %all-gather.9.cloned.1.call-done = bf16[4736,1792]{1,0:T(8,128)(2,1)} async-done(((bf16[296,1792]{1,0:T(8,128)(2,1)}), bf16[4736,1792]{1,0:T(8,128)(2,1)}) %all-gather.9.cloned.1.call-update) | async-done | bytes 16973840 | tf_op jit(solution)/shard_map/all_gather | solution.py:24
  206.3 12.7 %fusion.9 = f32[128,4736]{1,0:T(8,128)} fusion(bf16[128,1792]{1,0:T(8,128)(2,1)S(1)} %all_gather.22, bf16[4736,1792]{1,0:T(8,128)(2,1)} %all-gather.9.cloned.1.call-done), kind=kOutput, calls=%fused_computation.14 | convolution fusion | flops 2172649472 | bytes 19857408 | tf_op jit(solution)/shard_map/dot_general | solution.py:14
  219.1 181.1 %all-gather.5.cloned.1.call-done = bf16[4736,1792]{1,0:T(8,128)(2,1)} async-done(((bf16[296,1792]{1,0:T(8,128)(2,1)}), bf16[4736,1792]{1,0:T(8,128)(2,1)}) %all-gather.5.cloned.1.call-update) | async-done | bytes 16973840 | tf_op jit(solution)/shard_map/all_gather | solution.py:28
  400.1 12.7 %fusion.8 = f32[128,4736]{1,0:T(8,128)} fusion(bf16[128,1792]{1,0:T(8,128)(2,1)S(1)} %all_gather.20, bf16[4736,1792]{1,0:T(8,128)(2,1)} %all-gather.5.cloned.1.call-done), kind=kOutput, calls=%fused_computation.13 | convolution fusion | flops 2172649472 | bytes 19857408 | tf_op jit(solution)/shard_map/dot_general | solution.py:14
  412.9 181.1 %all-gather.7.cloned.1.call-done = bf16[4736,1792]{1,0:T(8,128)(2,1)} async-done(((bf16[296,1792]{1,0:T(8,128)(2,1)}), bf16[4736,1792]{1,0:T(8,128)(2,1)}) %all-gather.7.cloned.1.call-update) | async-done | bytes 16973840 | tf_op jit(solution)/shard_map/all_gather | solution.py:24
  594.0 0.0 copy-done
  594.0 12.8 %fusion.2 = bf16[128,4736]{1,0:T(8,128)(2,1)S(1)} fusion(f32[128,4736]{1,0:T(8,128)} %fusion.8, bf16[128,1792]{1,0:T(8,128)(2,1)S(1)} %all_gather.22, bf16[4736,1792]{1,0:T(8,128)(2,1)} %all-gather.7.cloned.1.call-done, f32[128,4736]{1,0:T(8,128)} %fusion.9), kind=kOutput, calls=%fused_computation.3 | convolution fusion | flops 2178711552 | bytes 23494656 | tf_op jit(solution)/shard_map/dot_general | solution.py:14
  606.8 0.0 copy-start.1
  606.8 0.0 copy-start.2
  606.8 0.0 copy-start.5
  606.8 8.4 %fusion.10 = f32[128,1792]{1,0:T(8,128)S(1)} fusion(bf16[128,4736]{1,0:T(8,128)(2,1)S(1)} %fusion.2, bf16[4736,1792]{1,0:T(8,128)(2,1)} %all-gather.9.cloned.1.call-done), kind=kOutput, calls=%fused_computation.15 | convolution fusion | flops 2172649472 | bytes 19103744 | tf_op jit(solution)/shard_map/dot_general | solution.py:39
  615.2 0.0 copy-done.1
  615.2 0.0 copy-done.2
  615.2 3.7 copy-done.5
  618.9 2.9 fusion.3
  621.8 1.0 copy.11
  622.8 0.0 reduce-scatter.4.cloned.1.call-update
  622.8 0.0 all-gather.11.cloned.1.call-start
  622.9 0.5 all-gather.11.cloned.1.call-update
  623.4 1.5 copy.9
  624.9 3.8 all-to-all-start
  628.8 0.3 reduce-scatter.4.cloned.1.call-done
  629.0 1.8 copy.12
  630.8 113.1 %all-gather.11.cloned.1.call-done = bf16[2048,1792]{1,0:T(8,128)(2,1)} async-done(((bf16[128,1792]{1,0:T(8,128)(2,1)}), bf16[2048,1792]{1,0:T(8,128)(2,1)}) %all-gather.11.cloned.1.call-update) | async-done | bytes 7340048 | tf_op jit(solution)/shard_map/all_gather | solution.py:34
  743.9 0.0 all-to-all-done
  743.9 6.4 convolution_convert_fusion
Async XLA Ops:
  7.2 2.3 copy-start.3
  7.2 4.5 copy-start.4
  7.2 199.2 %all-gather.9.cloned.1.call-start = ((), (), s32[]{:S(2)}) async-start(), calls=%async_computation.4 | async-start | bytes 18034688 | tf_op jit(solution)/shard_map/all_gather | solution.py:24
  7.9 392.2 %all-gather.5.cloned.1.call-start = ((), (), s32[]{:S(2)}) async-start(), calls=%async_computation.2 | async-start | bytes 18034688 | tf_op jit(solution)/shard_map/all_gather | solution.py:28
  8.7 585.3 %all-gather.7.cloned.1.call-start = ((), (), s32[]{:S(2)}) async-start(), calls=%async_computation.3 | async-start | bytes 18034688 | tf_op jit(solution)/shard_map/all_gather | solution.py:24
  9.4 619.6 %reduce-scatter.4.cloned.1.call-start = ((), (), s32[]{:S(2)}) async-start(), calls=%async_computation.6 | async-start | bytes 688128
  11.7 582.3 %copy-start = (bf16[128,1792]{1,0:T(8,128)(2,1)}, bf16[128,1792]{1,0:T(8,128)(2,1)S(1)}, u32[]{:S(2)}) copy-start(bf16[128,1792]{1,0:T(8,128)(2,1)S(1)} %all_gather.22) | copy-start | bytes 1376260
  606.8 8.4 %copy-start.1 = (f32[128,4736]{1,0:T(8,128)S(1)}, f32[128,4736]{1,0:T(8,128)}, u32[]{:S(2)}) copy-start(f32[128,4736]{1,0:T(8,128)} %fusion.9) | copy-start | bytes 7274500
  606.8 8.4 %copy-start.2 = (f32[128,4736]{1,0:T(8,128)S(1)}, f32[128,4736]{1,0:T(8,128)}, u32[]{:S(2)}) copy-start(f32[128,4736]{1,0:T(8,128)} %fusion.8) | copy-start | bytes 7274500
  606.8 12.1 %copy-start.5 = (bf16[4736,1792]{1,0:T(8,128)(2,1)S(1)}, bf16[4736,1792]{1,0:T(8,128)(2,1)}, u32[]{:S(2)}) copy-start(bf16[4736,1792]{1,0:T(8,128)(2,1)} %all-gather.7.cloned.1.call-done) | copy-start | bytes 50921476
  622.8 121.1 %all-gather.11.cloned.1.call-start = ((), (), s32[]{:S(2)}) async-start(), calls=%async_computation.5 | async-start | bytes 7798784 | tf_op jit(solution)/shard_map/all_gather | solution.py:34
  624.9 119.0 %all-to-all-start = ((bf16[128,16,296]{0,2,1:T(8,128)(2,1)}), bf16[128,16,296]{0,2,1:T(8,128)(2,1)S(1)}, u32[]{:S(2)}, u32[]{:S(2)}) async-start(bf16[128,16,296]{0,2,1:T(8,128)(2,1)} %bitcast), calls=%async_computation | async-start | bytes 2424832 | tf_op jit(solution)/shard_map/all_to_all | solution.py:33
Sparse Core Ops, SparseCore 0:
  10.7 195.6 all-gather.8
  209.0 191.0 all-gather.4
  402.8 191.0 all-gather.6
  622.9 6.0 reduce-scatter.3
  631.6 112.3 all-gather.10
where the time goes:
time: 757 us
  waiting for transfers between devices  671 us (89%)
  matrix products  55.9 us (7%)
  between operations  13.9 us (2%)
  local copies, waits for them, and re-layouts  7.97 us (1%)
    all_gather x2, waiting for transfers between devices, per_device(): pieces = lax.all_gather((gate_weight, up_weight), 'dp', axis=0, tiled=True)  374 us
    all_gather x1, waiting for transfers between devices, per_device(): lax.all_gather(down_weight, 'dp', axis=0, tiled=True)  181 us
    all_gather x1, waiting for transfers between devices, per_device(): gate_sum = tdot(owned, lax.all_gather(full_in, 'dp', axis=0, tiled=True))  113 us
    dot_general x3, matrix products, rdot(): lax.dot_general(left, right, (((1,), (1,)), ((), ())), preferred_element_...  38.2 us
  transfers between devices with their start and end apart: 6, of which 5 were waited for; matrix products, arithmetic and copies ran while one was open for 4% of the time, Pallas kernels for 0%

commit v1 on v0

v1 whole, which is shorter than its diff:
```python
import jax
import jax.numpy as jnp
from jax import lax
from jax.sharding import PartitionSpec as P


def tdot(left, right):
    return lax.dot_general(
        left, right, (((0,), (0,)), ((), ())), preferred_element_type=jnp.float32
    )


def rdot(left, right):
    return lax.dot_general(
        left, right, (((1,), (1,)), ((), ())), preferred_element_type=jnp.float32
    )


def per_device(inputs, cotangent, gate_weight, up_weight, down_weight):
    def tokens(block):
        rows = lax.all_gather(block, "dp", axis=0, tiled=True)
        return lax.all_gather(rows, "mp", axis=1, tiled=True)

    full_in = tokens(inputs)
    full_cot = tokens(cotangent)
    gate = rdot(full_in, gate_weight)
    up = rdot(full_in, up_weight)
    dhidden = rdot(full_cot, down_weight)
    sig = jax.nn.sigmoid(gate)
    act = gate * sig
    dup = (dhidden * act).astype(jnp.bfloat16)
    dgate = (dhidden * up * sig * (1.0 + gate * (1.0 - sig))).astype(jnp.bfloat16)
    partial = jnp.dot(dgate, gate_weight, preferred_element_type=jnp.float32)
    partial = partial + jnp.dot(dup, up_weight, preferred_element_type=jnp.float32)
    partial = lax.psum_scatter(
        partial.astype(jnp.bfloat16), "mp", scatter_dimension=1, tiled=True
    )
    input_grad = lax.psum_scatter(partial, "dp", scatter_dimension=0, tiled=True)
    gate_grad = tdot(dgate, full_in).astype(jnp.bfloat16)
    return (input_grad, gate_grad)


def solution(mesh):
    placed = (
        P("dp", "mp"),
        P("dp", "mp"),
        P(("mp", "dp"), None),
        P(("mp", "dp"), None),
        P(("mp", "dp"), None),
    )
    return jax.shard_map(
        per_device,
        mesh=mesh,
        in_specs=placed,
        out_specs=(P("dp", "mp"), P(("mp", "dp"), None)),
        check_vma=False,
    )
```

time: 757 us -> 351 us (0.46)
  waiting for transfers between devices: 671 us -> 281 us
  matrix products: 55.9 us -> 37.3 us
  local copies, waits for them, and re-layouts: 7.97 us -> 17.9 us
    all_gather x4, waiting for transfers between devices: 668 us -> 183 us  [the longest x2 149 us: tokens(): rows = lax.all_gather(block, 'dp', axis=0, tiled=True)]
    reduce_scatter x0 -> x1, waiting for transfers between devices: none -> 79.3 us  [per_device(): lax.psum_scatter(partial, 'dp', scatter_dimension=0, tiled=True)]
    dot_general x3, matrix products: 38.2 us -> 14.2 us  [rdot(): lax.dot_general(left, right, (((1,), (1,)), ((), ())), preferred_element_...]
    unnamed x6 -> x7, waiting for transfers between devices: 2.87 us -> 18.9 us
    unnamed x14, local copies, waits for them, and re-layouts: 6.43 us -> 17.9 us
  transfers between devices with their start and end apart: 6 -> 6, of which waited for: 5 -> 6; matrix products, arithmetic and copies ran while one was open for 4% -> 3% of each run, Pallas kernels for 0% -> 0%
where the time goes in v1:
time: 351 us; the launch traced here: 350 us
  waiting for transfers between devices  281 us (80%)
  matrix products  37.3 us (11%)
  local copies, waits for them, and re-layouts  17.9 us (5%)
  between operations  14.2 us (4%)
    all_gather x2, waiting for transfers between devices, tokens(): rows = lax.all_gather(block, 'dp', axis=0, tiled=True)  149 us
    reduce_scatter x1, waiting for transfers between devices, per_device(): lax.psum_scatter(partial, 'dp', scatter_dimension=0, tiled=True)  79.3 us
    all_gather x2, waiting for transfers between devices, tokens(): return lax.all_gather(rows, 'mp', axis=1, tiled=True)  33.4 us
    unnamed x7, waiting for transfers between devices  18.9 us
    unnamed x14, local copies, waits for them, and re-layouts  17.9 us
    dot_general x3, matrix products, rdot(): lax.dot_general(left, right, (((1,), (1,)), ((), ())), preferred_element_...  14.2 us
    dot_general x1, matrix products, per_device(): jnp.dot(dup, up_weight, preferred_element_type=jnp.float32)  9.27 us
    dot_general x1, matrix products, per_device(): partial = jnp.dot(dgate, gate_weight, preferred_element_type=jnp.float32)  7.38 us
  transfers between devices with their start and end apart: 6, of which 6 were waited for; matrix products, arithmetic and copies ran while one was open for 3% of the time, Pallas kernels for 0%

profile of v1, /device:TPU:0, one launch (start us, length us, event | category | flops | bytes accessed | tf_op | source)
XLA Modules:
  0.0 350.5 jit_solution(10456565937666532263)
XLA Ops:
  7.2 0.0 copy-start
  7.2 0.0 all-gather.5.cloned.1.call-start
  7.2 0.7 all-gather.5.cloned.1.call-update
  7.9 0.0 all-gather.9.cloned.1.call-start
  8.0 0.7 all-gather.9.cloned.1.call-update
  8.7 0.0 all-gather.7.cloned.1.call-start
  8.7 76.4 %all-gather.5.cloned.1.call-done = bf16[2048,896]{1,0:T(8,128)(2,1)} async-done(((bf16[128,896]{1,0:T(8,128)(2,1)}), bf16[2048,896]{1,0:T(8,128)(2,1)}) %all-gather.5.cloned.1.call-update) | async-done | bytes 3670032 | tf_op jit(solution)/shard_map/all_gather | solution.py:21
  85.1 0.0 all-gather.7.cloned.1.call-update
  85.1 0.0 all-gather.11.cloned.1.call-start
  85.2 72.9 %all-gather.9.cloned.1.call-done = bf16[2048,896]{1,0:T(8,128)(2,1)} async-done(((bf16[128,896]{1,0:T(8,128)(2,1)}), bf16[2048,896]{1,0:T(8,128)(2,1)}) %all-gather.9.cloned.1.call-update) | async-done | bytes 3670032 | tf_op jit(solution)/shard_map/all_gather | solution.py:21
  158.1 0.0 all-gather.11.cloned.1.call-update
  158.1 0.0 reduce-scatter.7.cloned.1.call-start
  158.1 18.3 %all-gather.7.cloned.1.call-done = bf16[2048,1792]{1,0:T(8,128)(2,1)} async-done(((bf16[2048,896]{1,0:T(8,128)(2,1)}), bf16[2048,1792]{1,0:T(8,128)(2,1)}) %all-gather.7.cloned.1.call-update) | async-done | bytes 7340048 | tf_op jit(solution)/shard_map/all_gather | solution.py:22
  176.4 5.7 %fusion.5 = f32[2048,296]{0,1:T(8,128)S(1)} fusion(bf16[2048,1792]{1,0:T(8,128)(2,1)} %all-gather.7.cloned.1.call-done, bf16[296,1792]{1,0:T(8,128)(2,1)} %param.9), kind=kOutput, calls=%fused_computation.10 | convolution fusion | flops 2172649472 | bytes 10825728 | tf_op jit(solution)/shard_map/dot_general | solution.py:14
  182.1 15.1 %all-gather.11.cloned.1.call-done = bf16[2048,1792]{1,0:T(8,128)(2,1)} async-done(((bf16[2048,896]{1,0:T(8,128)(2,1)}), bf16[2048,1792]{1,0:T(8,128)(2,1)}) %all-gather.11.cloned.1.call-update) | async-done | bytes 7340048 | tf_op jit(solution)/shard_map/all_gather | solution.py:22
  197.2 0.0 copy-done
  197.2 0.0 copy-start.4
  197.2 0.0 copy-start.5
  197.2 5.6 %fusion.6 = f32[2048,296]{0,1:T(8,128)S(1)} fusion(bf16[2048,1792]{1,0:T(8,128)(2,1)} %all-gather.11.cloned.1.call-done, bf16[296,1792]{1,0:T(8,128)(2,1)S(1)} %copy-done), kind=kOutput, calls=%fused_computation.11 | convolution fusion | flops 2172649472 | bytes 10825728 | tf_op jit(solution)/shard_map/dot_general | solution.py:14
  202.9 0.0 copy-done.4
  202.9 0.0 copy-done.5
  202.9 2.8 fusion.2
  205.7 0.0 copy-start.2
  205.7 7.4 %fusion.7 = f32[2048,1792]{1,0:T(8,128)} fusion(bf16[2048,296]{0,1:T(8,128)(2,1)S(1)} %fusion.2, bf16[296,1792]{1,0:T(8,128)(2,1)S(1)} %copy-done), kind=kOutput, calls=%fused_computation.12 | convolution fusion | flops 2172649472 | bytes 16953344 | tf_op jit(solution)/shard_map/dot_general | solution.py:33
  213.1 0.0 copy-done.2
  213.1 9.3 %add_convert_fusion = bf16[2048,1792]{1,0:T(8,128)(2,1)} fusion(f32[2048,1792]{1,0:T(8,128)} %fusion.7, bf16[296,1792]{1,0:T(8,128)(2,1)S(1)} %copy-done.4, f32[2048,296]{0,1:T(8,128)S(1)} %fusion.5, f32[2048,296]{0,1:T(8,128)S(1)} %fusion.6), kind=kOutput, calls=%fused_computation | convolution fusion | flops 2183626752 | bytes 27930624 | tf_op jit(solution)/shard_map/dot_general | solution.py:34
  222.4 10.5 %copy.7 = bf16[2048,1792]{0,1:T(8,128)(2,1)} copy(bf16[2048,1792]{1,0:T(8,128)(2,1)} %add_convert_fusion) | data formatting | bytes 14680064
  232.9 0.0 reduce-scatter.7.cloned.1.call-update
  232.9 0.0 reduce-scatter.5.cloned.1.call-start
  233.0 17.4 %reduce-scatter.7.cloned.1.call-done = bf16[896,2048]{1,0:T(8,128)(2,1)} async-done(((bf16[1792,2048]{1,0:T(8,128)(2,1)}), bf16[896,2048]{1,0:T(8,128)(2,1)}) %reduce-scatter.7.cloned.1.call-update) | async-done | bytes 3670032
  250.4 6.1 %copy.8 = bf16[2048,896]{1,0:T(8,128)(2,1)} copy(bf16[2048,896]{0,1:T(8,128)(2,1)} %bitcast.14) | data formatting | bytes 7340032
  256.5 0.0 copy-start.3
  256.5 0.0 reduce-scatter.5.cloned.1.call-update
  256.5 1.3 copy-done.3
  257.8 0.0 copy-start.1
  257.8 6.5 %convolution_convert_fusion = bf16[296,1792]{1,0:T(8,128)(2,1)} fusion(bf16[2048,296]{0,1:T(8,128)(2,1)S(1)} %copy-done.3, bf16[2048,1792]{1,0:T(8,128)(2,1)} %all-gather.11.cloned.1.call-done), kind=kOutput, calls=%fused_computation.5 | convolution fusion | flops 2173179904 | bytes 9613312 | tf_op jit(solution)/shard_map/dot_general | solution.py:8
  264.3 79.3 %reduce-scatter.5.cloned.1.call-done = bf16[128,896]{1,0:T(8,128)(2,1)} async-done(((bf16[2048,896]{1,0:T(8,128)(2,1)}), bf16[128,896]{1,0:T(8,128)(2,1)}) %reduce-scatter.5.cloned.1.call-update) | async-done | bytes 229392 | tf_op jit(solution)/shard_map/reduce_scatter | solution.py:38
  343.6 0.0 copy-done.1
Async XLA Ops:
  7.2 190.1 %copy-start = (bf16[296,1792]{1,0:T(8,128)(2,1)S(1)}, bf16[296,1792]{1,0:T(8,128)(2,1)}, u32[]{:S(2)}) copy-start(bf16[296,1792]{1,0:T(8,128)(2,1)} %param.7) | copy-start | bytes 3182596
  7.2 77.9 %all-gather.5.cloned.1.call-start = ((), (), s32[]{:S(2)}) async-start(), calls=%async_computation.2 | async-start | bytes 3899392 | tf_op jit(solution)/shard_map/all_gather | solution.py:21
  7.9 150.2 %all-gather.9.cloned.1.call-start = ((), (), s32[]{:S(2)}) async-start(), calls=%async_computation.4 | async-start | bytes 3899392 | tf_op jit(solution)/shard_map/all_gather | solution.py:21
  8.7 167.7 %all-gather.7.cloned.1.call-start = ((), (), s32[]{:S(2)}) async-start(), calls=%async_computation.3 | async-start | bytes 11010048 | tf_op jit(solution)/shard_map/all_gather | solution.py:22
  85.1 112.1 %all-gather.11.cloned.1.call-start = ((), (), s32[]{:S(2)}) async-start(), calls=%async_computation.5 | async-start | bytes 11010048 | tf_op jit(solution)/shard_map/all_gather | solution.py:22
  158.1 92.3 %reduce-scatter.7.cloned.1.call-start = ((), (), s32[]{:S(2)}) async-start(), calls=%async_computation.7 | async-start | bytes 11010048
  197.2 5.6 %copy-start.4 = (bf16[296,1792]{1,0:T(8,128)(2,1)S(1)}, bf16[296,1792]{1,0:T(8,128)(2,1)}, u32[]{:S(2)}) copy-start(bf16[296,1792]{1,0:T(8,128)(2,1)} %param.8) | copy-start | bytes 3182596
  197.2 5.6 %copy-start.5 = (bf16[2048,1792]{1,0:T(8,128)(2,1)S(1)}, bf16[2048,1792]{1,0:T(8,128)(2,1)}, u32[]{:S(2)}) copy-start(bf16[2048,1792]{1,0:T(8,128)(2,1)} %all-gather.11.cloned.1.call-done) | copy-start | bytes 22020100
  205.7 7.4 %copy-start.2 = (bf16[2048,296]{0,1:T(8,128)(2,1)}, bf16[2048,296]{0,1:T(8,128)(2,1)S(1)}, u32[]{:S(2)}) copy-start(bf16[2048,296]{0,1:T(8,128)(2,1)S(1)} %fusion.2) | copy-start | bytes 3637252
  232.9 110.7 %reduce-scatter.5.cloned.1.call-start = ((), (), s32[]{:S(2)}) async-start(), calls=%async_computation.6 | async-start | bytes 3899392 | tf_op jit(solution)/shard_map/reduce_scatter | solution.py:38
  256.5 1.3 copy-start.3
  257.8 85.9 %copy-start.1 = (bf16[296,1792]{1,0:T(8,128)(2,1)S(1)}, bf16[296,1792]{1,0:T(8,128)(2,1)}, u32[]{:S(2)}) copy-start(bf16[296,1792]{1,0:T(8,128)(2,1)} %param.7) | copy-start | bytes 3182596
Sparse Core Ops, SparseCore 0:
  10.7 74.3 all-gather.4
  87.9 70.1 all-gather.8
  159.6 16.7 all-gather.6
  177.8 19.3 all-gather.10
  233.0 17.3 reduce-scatter.6
  256.6 86.9 reduce-scatter.4

commit v2 on v1

v2 whole, which is shorter than its diff:
```python
import functools

import jax
import jax.numpy as jnp
from jax import lax
from jax.experimental import pallas as pl
from jax.experimental.pallas import tpu as pltpu
from jax.sharding import PartitionSpec as P

F32 = jnp.float32
BF16 = jnp.bfloat16
VMEM_LIMIT = 63 * 1024 * 1024


def tdot(left, right):
    return lax.dot_general(
        left, right, (((0,), (0,)), ((), ())), preferred_element_type=F32
    )


def rdot(left, right):
    return lax.dot_general(
        left, right, (((1,), (1,)), ((), ())), preferred_element_type=F32
    )


def gradients(gate, up, dhidden):
    sig = jax.nn.sigmoid(gate)
    act = gate * sig
    dup = (dhidden * act).astype(BF16)
    dgate = (dhidden * up * sig * (1.0 + gate * (1.0 - sig))).astype(BF16)
    return dgate, dup


def by_collectives(inputs, cotangent, gate_weight, up_weight, down_weight):
    def tokens(block):
        rows = lax.all_gather(block, "dp", axis=0, tiled=True)
        return lax.all_gather(rows, "mp", axis=1, tiled=True)

    full_in = tokens(inputs)
    full_cot = tokens(cotangent)
    dgate, dup = gradients(
        rdot(full_in, gate_weight),
        rdot(full_in, up_weight),
        rdot(full_cot, down_weight),
    )
    partial = jnp.dot(dgate, gate_weight, preferred_element_type=F32)
    partial = partial + jnp.dot(dup, up_weight, preferred_element_type=F32)
    partial = lax.psum_scatter(
        partial.astype(BF16), "mp", scatter_dimension=1, tiled=True
    )
    input_grad = lax.psum_scatter(partial, "dp", scatter_dimension=0, tiled=True)
    return input_grad, tdot(dgate, full_in).astype(BF16)


def kernel(
    nz,
    in_ref,
    cot_ref,
    gw,
    uw,
    dw,
    ig_ref,
    gg_ref,
    tok,
    dgt,
    mine,
    give,
    took,
    r1,
    r2,
    r3,
    ag_send,
    ag_recv,
    swap_send,
    swap_recv,
    s1_send,
    s1_recv,
    s2_send,
    s2_recv,
    s3_send,
    s3_recv,
):
    rows, wide = in_ref.shape
    half_rows = rows // 2
    d = lax.axis_index("dp")
    c = lax.axis_index("mp")
    z, r = d // 4, d % 4
    y, x = r // 2, r % 2
    other = 1 - c
    own_rank = r
    x_rank, y_rank, far_rank = y * 2 + 1 - x, (1 - y) * 2 + x, (1 - y) * 2 + 1 - x
    peer, xn, yn = (d, other), (z * 4 + x_rank, c), (z * 4 + y_rank, c)

    def column(k):
        return (((z + k) % nz) * 4 + r, c)

    barrier = pltpu.get_barrier_semaphore()
    friends = [peer, xn, yn] + [column(k) for k in range(1, nz)]
    for friend in friends:
        pl.semaphore_signal(
            barrier, inc=1, device_id=friend, device_id_type=pl.DeviceIdType.MESH
        )
    pl.semaphore_wait(barrier, len(friends))

    sent = []

    def send(src, dst, send_sem, recv_sem, device):
        copy = pltpu.make_async_remote_copy(
            src_ref=src,
            dst_ref=dst,
            send_sem=send_sem,
            recv_sem=recv_sem,
            device_id=device,
            device_id_type=pl.DeviceIdType.MESH,
        )
        copy.start()
        sent.append(copy)

    def arrive(dst, send_sem, recv_sem):
        pltpu.make_async_remote_copy(
            src_ref=dst,
            dst_ref=dst,
            send_sem=send_sem,
            recv_sem=recv_sem,
            device_id=peer,
            device_id_type=pl.DeviceIdType.MESH,
        ).wait_recv()

    count = [0, 0]

    def pass_on(a, slot, device, src=None, half=c):
        src = tok.at[a, half, slot] if src is None else src
        send(
            src,
            tok.at[a, half, slot],
            ag_send.at[a, count[a]],
            ag_recv.at[a, half, slot],
            device,
        )
        count[a] += 1

    def landed(a, half, slot):
        arrive(tok.at[a, half, slot], ag_send.at[a, 0], ag_recv.at[a, half, slot])

    sources = (in_ref, cot_ref)
    first, second = (xn, yn), (yn, xn)
    first_rank, second_rank = (x_rank, y_rank), (y_rank, x_rank)

    def layer(k):
        return (z + nz - k) % nz

    for a in range(2):
        pass_on(a, d, first[a], sources[a])
    for k in range(1, nz):
        for a in range(2):
            pass_on(a, d, column(k), sources[a])
    for a in range(2):
        pass_on(a, d, second[a], sources[a])
    for a in range(2):
        pass_on(a, d, peer, sources[a])
    for a in range(2):
        tok[a, c, d] = sources[a][...]

    def from_column(k):
        slot = layer(k) * 4 + own_rank
        for a in range(2):
            landed(a, c, slot)
            pass_on(a, slot, first[a])
            pass_on(a, slot, second[a])
            pass_on(a, slot, peer)

    def from_first(k):
        for a in range(2):
            slot = layer(k) * 4 + first_rank[a]
            landed(a, c, slot)
            pass_on(a, slot, second[a])
            pass_on(a, slot, peer)

    def from_second(k):
        for a in range(2):
            slot = layer(k) * 4 + second_rank[a]
            landed(a, c, slot)
            pass_on(a, slot, peer)
        for a in range(2):
            slot = layer(k) * 4 + far_rank
            landed(a, c, slot)
            pass_on(a, slot, peer)

    own_columns = pl.ds(pl.multiple_of(c * wide, 128), wide)
    other_columns = pl.ds(pl.multiple_of(other * wide, 128), wide)

    def compute(k):
        base = layer(k) * 4
        for rank in (own_rank, x_rank, y_rank, far_rank):
            for a in range(2):
                landed(a, other, base + rank)

        @pl.loop(0, 2)
        def _(j):
            s = base + 2 * j

            def project(weight, a):
                total = None
                for h in range(2):
                    block = tok[a, h, pl.ds(s, 2)].reshape(2 * rows, wide)
                    part = rdot(weight[:, h * wide : (h + 1) * wide], block)
                    total = part if total is None else total + part
                return total

            dgate, dup = gradients(project(gw, 0), project(uw, 0), project(dw, 1))
            dgt[:, pl.ds(pl.multiple_of(s * rows, 128), 2 * rows)] = dgate
            for target, columns in ((give, other_columns), (mine, own_columns)):
                part = tdot(dgate, gw[:, columns]) + tdot(dup, uw[:, columns])
                target[pl.ds(s, 2)] = part.astype(BF16).reshape(2, rows, wide)

        group = pl.ds(base, 4)
        send(give.at[group], took.at[group], swap_send.at[k], swap_recv.at[k], peer)

    top, low = pl.ds(0, half_rows), pl.ds(half_rows, half_rows)

    def add(buffer, extra, slot, part):
        total = buffer[slot, part].astype(F32) + extra[slot, part].astype(F32)
        buffer[slot, part] = total.astype(BF16)

    def stage1(k):
        base = layer(k) * 4
        group = pl.ds(base, 4)
        arrive(took.at[group], swap_send.at[k], swap_recv.at[k])

        @pl.loop(0, 4)
        def _(j):
            add(mine, took, base + j, pl.ds(0, rows))

        for i, (part, ranks, device) in enumerate(
            ((top, (far_rank, x_rank), xn), (low, (far_rank, y_rank), yn))
        ):
            for n, rank in enumerate(ranks):
                piece = (base + rank, part)
                send(
                    mine.at[piece],
                    r1.at[piece],
                    s1_send.at[k, i, n],
                    s1_recv.at[k, i, n],
                    device,
                )

    def stage2(k):
        base = layer(k) * 4
        for n in range(2):
            for i, (part, far, device) in enumerate(
                ((top, y_rank, yn), (low, x_rank, xn))
            ):
                piece = (base + (far, own_rank)[n], part)
                arrive(r1.at[piece], s1_send.at[k, i, n], s1_recv.at[k, i, n])
                add(mine, r1, *piece)
                if n == 0:
                    send(
                        mine.at[piece],
                        r2.at[piece],
                        s2_send.at[k, i],
                        s2_recv.at[k, i],
                        device,
                    )

    def stage3(k):
        slot = layer(k) * 4 + own_rank
        for i, part in enumerate((top, low)):
            arrive(r2.at[slot, part], s2_send.at[k, i], s2_recv.at[k, i])
            add(mine, r2, slot, part)
        if k > 0:
            send(
                mine.at[slot],
                r3.at[k],
                s3_send.at[k],
                s3_recv.at[k],
                ((z + nz - k) % nz * 4 + r, c),
            )

    def weight_gradient(h):
        block = tok[0, h].reshape(-1, wide)
        grad = jnp.dot(dgt[...], block, preferred_element_type=F32)
        gg_ref[:, h * wide : (h + 1) * wide] = grad.astype(BF16)

    for k in range(nz):
        from_first(k)
        if k + 1 < nz:
            from_column(k + 1)
        from_second(k)
        if k >= 1:
            stage1(k - 1)
        if k >= 2:
            stage2(k - 2)
        if k >= 3:
            stage3(k - 3)
        compute(k)
    last = nz - 1
    if nz >= 2:
        stage2(last - 1)
    if nz >= 3:
        stage3(last - 2)
    stage1(last)
    if nz >= 2:
        stage3(last - 1)
    weight_gradient(0)
    stage2(last)
    weight_gradient(1)
    stage3(last)
    total = mine[d].astype(F32)
    for k in range(1, nz):
        arrive(r3.at[k], s3_send.at[k], s3_recv.at[k])
        total = total + r3[k].astype(F32)
    ig_ref[...] = total.astype(BF16)
    for copy in sent:
        copy.wait_send()


def by_kernel(n, inputs, cotangent, gate_weight, up_weight, down_weight):
    rows, wide = inputs.shape
    hidden, features = gate_weight.shape
    nz = n // 4
    sends = 2 * n
    dma = pltpu.SemaphoreType.DMA
    whole = pltpu.VMEM((n, rows, wide), BF16)
    return pl.pallas_call(
        functools.partial(kernel, nz),
        out_shape=(
            jax.ShapeDtypeStruct((rows, wide), BF16),
            jax.ShapeDtypeStruct((hidden, features), BF16),
        ),
        in_specs=[pl.BlockSpec(memory_space=pltpu.VMEM)] * 5,
        out_specs=[pl.BlockSpec(memory_space=pltpu.VMEM)] * 2,
        scratch_shapes=[
            pltpu.VMEM((2, 2, n, rows, wide), BF16),
            pltpu.VMEM((hidden, n * rows), BF16),
            whole,
            whole,
            whole,
            whole,
            whole,
            pltpu.VMEM((nz, rows, wide), BF16),
            dma((2, sends)),
            dma((2, 2, n)),
            dma((nz,)),
            dma((nz,)),
            dma((nz, 2, 2)),
            dma((nz, 2, 2)),
            dma((nz, 2)),
            dma((nz, 2)),
            dma((nz,)),
            dma((nz,)),
        ],
        compiler_params=pltpu.CompilerParams(
            collective_id=0, has_side_effects=True, vmem_limit_bytes=VMEM_LIMIT
        ),
    )(inputs, cotangent, gate_weight, up_weight, down_weight)


def solution(mesh):
    n, cores = mesh.shape["dp"], mesh.shape["mp"]

    def per_device(inputs, cotangent, gate_weight, up_weight, down_weight):
        rows, wide = inputs.shape
        hidden, features = gate_weight.shape
        held = 2 * (9 * n * rows * wide + 5 * hidden * features + hidden * n * rows)
        fits = held <= VMEM_LIMIT * 3 // 4
        even = n % 4 == 0 and rows % 64 == 0 and wide % 128 == 0
        args = (inputs, cotangent, gate_weight, up_weight, down_weight)
        if cores == 2 and fits and even:
            return tuple(by_kernel(n, *args))
        return by_collectives(*args)

    placed = (
        P("dp", "mp"),
        P("dp", "mp"),
        P(("mp", "dp"), None),
        P(("mp", "dp"), None),
        P(("mp", "dp"), None),
    )
    return jax.shard_map(
        per_device,
        mesh=mesh,
        in_specs=placed,
        out_specs=(P("dp", "mp"), P(("mp", "dp"), None)),
        check_vma=False,
    )
```

time: 351 us -> 130 us (0.37)
  waiting for transfers between devices: 281 us -> 0 us
  Pallas kernels: 0 us -> 125 us
  matrix products: 37.3 us -> 0 us
  local copies, waits for them, and re-layouts: 17.9 us -> 3.92 us
  between operations: 14.2 us -> 0.64 us
    all_gather x4 -> x0, waiting for transfers between devices: 183 us -> none  [the longest x2 149 us: tokens(): rows = lax.all_gather(block, 'dp', axis=0, tiled=True)]
    pallas_call x0 -> x1, Pallas kernels: none -> 125 us  [by_kernel(): pl.pallas_call(functools.partial(kernel, nz), out_shape=(jax.ShapeDtypeSt...]
    reduce_scatter x1 -> x0, waiting for transfers between devices: 79.3 us -> none  [per_device(): lax.psum_scatter(partial, 'dp', scatter_dimension=0, tiled=True)]
    dot_general x6 -> x0, matrix products: 37.3 us -> none  [the longest x3 14.2 us: rdot(): lax.dot_general(left, right, (((1,), (1,)), ((), ())), preferred_element_...]
    unnamed x7 -> x0, waiting for transfers between devices: 18.9 us -> none
    unnamed x14 -> x2, local copies, waits for them, and re-layouts: 17.9 us -> 3.92 us
  transfers between devices with their start and end apart: 6 -> 0, of which waited for: 6 -> 0; matrix products, arithmetic and copies ran while one was open for 3% -> 0% of each run, Pallas kernels for 0% -> 0%
where the time goes in v2:
time: 130 us
  Pallas kernels  125 us (96%)
  local copies, waits for them, and re-layouts  3.92 us (3%)
    pallas_call x1, Pallas kernels, by_kernel(): pl.pallas_call(functools.partial(kernel, nz), out_shape=(jax.ShapeDtypeSt...  125 us
    unnamed x2, local copies, waits for them, and re-layouts  3.92 us

profile of v2, /device:TPU:0, one launch (start us, length us, event | category | flops | bytes accessed | tf_op | source)
XLA Modules:
  0.0 129.7 jit_solution(15040482271743267875)
XLA Ops:
  0.6 125.1 %shard_map.68 = (bf16[128,896]{1,0:T(8,128)(2,1)}, bf16[296,1792]{1,0:T(8,128)(2,1)}) custom-call(bf16[128,896]{1,0:T(8,128)(2,1)} %in_ref.1, bf16[128,896]{1,0:T(8,128)(2,1)} %cot_ref.1, bf16[296,1792]{1,0:T(8,128)(2,1)} %gw.1, bf16[296,1792]{1,0:T(8,128)(2,1)} %uw.1, bf16[296,1792]{1,0:T(8,128)(2,1)} %dw.1), custom_call_target="tpu_custom_call" | custom-call | tf_op jit(solution)/shard_map/pallas_call | solution.py:325
  125.7 1.6 %copy.9 = bf16[128,896]{1,0:T(8,128)(2,1)} copy(bf16[128,896]{1,0:T(8,128)(2,1)} %get-tuple-element.4) | data formatting | bytes 458752
  127.4 2.3 %copy.10 = bf16[296,1792]{1,0:T(8,128)(2,1)} copy(bf16[296,1792]{1,0:T(8,128)(2,1)} %get-tuple-element.5) | data formatting | bytes 2121728

commit v3 on v2

--- a/solution.py
+++ b/solution.py
@@ -57,11 +57,14 @@
     nz,
     in_ref,
     cot_ref,
+    gw_ref,
+    uw_ref,
+    dw_ref,
+    ig_ref,
+    gg_ref,
     gw,
     uw,
     dw,
-    ig_ref,
-    gg_ref,
     tok,
     dgt,
     mine,
@@ -80,6 +83,7 @@
     s2_recv,
     s3_send,
     s3_recv,
+    load_sem,
 ):
     rows, wide = in_ref.shape
     half_rows = rows // 2
@@ -94,6 +98,13 @@
 
     def column(k):
         return (((z + k) % nz) * 4 + r, c)
+
+    loads = [
+        pltpu.make_async_copy(source, held, load_sem.at[i])
+        for i, (source, held) in enumerate(((gw_ref, gw), (uw_ref, uw), (dw_ref, dw)))
+    ]
+    for load in loads:
+        load.start()
 
     barrier = pltpu.get_barrier_semaphore()
     friends = [peer, xn, yn] + [column(k) for k in range(1, nz)]
@@ -293,6 +304,9 @@
             stage2(k - 2)
         if k >= 3:
             stage3(k - 3)
+        if k == 0:
+            for load in loads:
+                load.wait()
         compute(k)
     last = nz - 1
     if nz >= 2:
@@ -328,9 +342,11 @@
             jax.ShapeDtypeStruct((rows, wide), BF16),
             jax.ShapeDtypeStruct((hidden, features), BF16),
         ),
-        in_specs=[pl.BlockSpec(memory_space=pltpu.VMEM)] * 5,
+        in_specs=[pl.BlockSpec(memory_space=pltpu.VMEM)] * 2
+        + [pl.BlockSpec(memory_space=pl.ANY)] * 3,
         out_specs=[pl.BlockSpec(memory_space=pltpu.VMEM)] * 2,
-        scratch_shapes=[
+        scratch_shapes=[pltpu.VMEM((hidden, features), BF16)] * 3
+        + [
             pltpu.VMEM((2, 2, n, rows, wide), BF16),
             pltpu.VMEM((hidden, n * rows), BF16),
             whole,
@@ -349,6 +365,7 @@
             dma((nz, 2)),
             dma((nz,)),
             dma((nz,)),
+            dma((3,)),
         ],
         compiler_params=pltpu.CompilerParams(
             collective_id=0, has_side_effects=True, vmem_limit_bytes=VMEM_LIMIT

time: 130 us -> 129 us (level)
  no operation moved by 1% of the time
where the time goes in v3:
time: 129 us
  Pallas kernels  124 us (96%)
  local copies, waits for them, and re-layouts  3.92 us (3%)
    pallas_call x1, Pallas kernels, by_kernel(): pl.pallas_call(functools.partial(kernel, nz), out_shape=(jax.ShapeDtypeSt...  124 us
    unnamed x2, local copies, waits for them, and re-layouts  3.92 us

profile of v3, /device:TPU:0, one launch (start us, length us, event | category | flops | bytes accessed | tf_op | source)
XLA Modules:
  0.0 128.7 jit_solution(7563404157410611820)
XLA Ops:
  0.6 124.1 %shard_map.68 = (bf16[128,896]{1,0:T(8,128)(2,1)}, bf16[296,1792]{1,0:T(8,128)(2,1)}) custom-call(bf16[128,896]{1,0:T(8,128)(2,1)} %in_ref.1, bf16[128,896]{1,0:T(8,128)(2,1)} %cot_ref.1, bf16[296,1792]{1,0:T(8,128)(2,1)} %gw_ref.1, bf16[296,1792]{1,0:T(8,128)(2,1)} %uw_ref.1, bf16[296,1792]{1,0:T(8,128)(2,1)} %dw_ref.1), custom_call_target="tpu_custom_call" | custom-call | tf_op jit(solution)/shard_map/pallas_call | solution.py:339
  124.8 1.6 %copy.9 = bf16[128,896]{1,0:T(8,128)(2,1)} copy(bf16[128,896]{1,0:T(8,128)(2,1)} %get-tuple-element.4) | data formatting | bytes 458752
  126.4 2.3 %copy.10 = bf16[296,1792]{1,0:T(8,128)(2,1)} copy(bf16[296,1792]{1,0:T(8,128)(2,1)} %get-tuple-element.5) | data formatting | bytes 2121728
